TPU v7x, 32 devices: a whole 2x2x4 slice. The times are simulated.
32 devices in a mesh: lat: 8 (over z, y), lon: 4 (over x, core).
Axes of the slice: x: 2, y: 2, z: 4, core: 2. Of those that a mesh axis runs over, the one named last changes fastest.
Arguments:
- predicted_state: bfloat16 [222, 320, 512], P(None, 'lat', 'lon'), may hold values from -30 to 30
- observed_state: bfloat16 [222, 320, 512], P(None, 'lat', 'lon'), may hold values from -30 to 30
- longterm_average_state: bfloat16 [222, 320, 512], P(None, 'lat', 'lon'), may hold values from -30 to 30
Outputs:
- blurred_mismatch_map: bfloat16 [222, 320, 512], P(None, 'lat', 'lon')
- quadratic_mean_mistake: float32 [222], replicated
- pattern_agreement: float32 [222], replicated
All inputs are finite; a program needn't handle non-finite values.
Results may differ from a plain program's by a relative error of at most 0.00155.
Values may be sent and summed in bfloat16 or wider, within the bound.
A program may use at most 128 MiB of HBM per device.

v0:
```python
import jax
import jax.numpy as jnp
from jax import lax
from jax.sharding import PartitionSpec as P

epsilon = 1e-06


def extended(cells, sides, width):
    for axis, dim in sides:
        count = lax.axis_size(axis)
        head = lax.slice_in_dim(cells, 0, width, axis=dim)
        tail = lax.slice_in_dim(cells, cells.shape[dim] - width, cells.shape[dim], axis=dim)
        cells = jnp.concatenate(
            [
                lax.ppermute(tail, axis, [(i, (i + 1) % count) for i in range(count)]),
                cells,
                lax.ppermute(head, axis, [((i + 1) % count, i) for i in range(count)]),
            ],
            axis=dim,
        )
    return cells


def deviation_from_normal(predicted_state, observed_state, longterm_average_state):
    normal_reference_state = longterm_average_state.astype(jnp.float32)
    return (
        predicted_state.astype(jnp.float32) - normal_reference_state,
        observed_state.astype(jnp.float32) - normal_reference_state,
    )


def vertical_sum(member):
    return member[:, :-2] + member[:, 1:-1] + member[:, 2:]


def horizontal_sum(member):
    return member[:, :, :-2] + member[:, :, 1:-1] + member[:, :, 2:]


def finish(running_accumulations, grid_cells):
    mean_fcst = running_accumulations[1] / grid_cells
    mean_true = running_accumulations[2] / grid_cells
    variance_fcst = running_accumulations[3] / grid_cells - mean_fcst * mean_fcst
    variance_true = running_accumulations[4] / grid_cells - mean_true * mean_true
    covariance = running_accumulations[5] / grid_cells - mean_fcst * mean_true
    quadratic_mean_mistake = jnp.sqrt(running_accumulations[0] / grid_cells)
    pattern_agreement = covariance / jnp.sqrt((variance_fcst + epsilon) * (variance_true + epsilon))
    return (quadratic_mean_mistake, pattern_agreement)


def local(predicted_state, observed_state, longterm_average_state):
    nearby_parallel_accumulated = predicted_state.shape[1]
    parallel_overall_accumulated = nearby_parallel_accumulated * lax.axis_size("lat")
    meridian_accumulated = predicted_state.shape[2] * lax.axis_size("lon")
    row_start = lax.axis_index("lat") * nearby_parallel_accumulated
    row_index = row_start + jnp.arange(nearby_parallel_accumulated, dtype=jnp.int32)
    stacked_inputs = jnp.stack([predicted_state, observed_state, longterm_average_state])
    rimmed = extended(stacked_inputs, (("lat", 2), ("lon", 3)), 1)
    widened = deviation_from_normal(rimmed[0], rimmed[1], rimmed[2])
    padded_index = row_start - 1 + jnp.arange(nearby_parallel_accumulated + 2, dtype=jnp.int32)
    inside = ((padded_index >= 0) & (padded_index < parallel_overall_accumulated)).astype(
        jnp.float32
    )[None, :, None]
    summed = tuple((horizontal_sum(vertical_sum(member * inside)) for member in widened))
    row_count = (
        3.0
        - (row_index == 0).astype(jnp.float32)
        - (row_index == parallel_overall_accumulated - 1).astype(jnp.float32)
    )
    divisor = (3.0 * row_count)[:, None]
    averaged_prediction = summed[0] / divisor
    averaged_observation = summed[1] / divisor
    prediction_mismatch = averaged_prediction - averaged_observation
    all_rows = jnp.arange(parallel_overall_accumulated, dtype=jnp.float32)
    cosine = jnp.cos(jnp.pi * (0.5 - all_rows / (parallel_overall_accumulated - 1)))
    weight_all = cosine / jnp.mean(cosine)
    cosine_factor_vector = lax.dynamic_slice_in_dim(
        weight_all, row_start, nearby_parallel_accumulated
    )[:, None]
    weighted_fcst = cosine_factor_vector * averaged_prediction
    weighted_true = cosine_factor_vector * averaged_observation
    running_accumulations = jnp.stack(
        [
            jnp.sum(cosine_factor_vector * prediction_mismatch * prediction_mismatch, axis=(1, 2)),
            jnp.sum(weighted_fcst, axis=(1, 2)),
            jnp.sum(weighted_true, axis=(1, 2)),
            jnp.sum(weighted_fcst * averaged_prediction, axis=(1, 2)),
            jnp.sum(weighted_true * averaged_observation, axis=(1, 2)),
            jnp.sum(weighted_fcst * averaged_observation, axis=(1, 2)),
        ]
    )
    totals = lax.psum(running_accumulations, ("lat", "lon"))
    quadratic_mean_mistake, pattern_agreement = finish(
        totals, float(parallel_overall_accumulated * meridian_accumulated)
    )
    return (prediction_mismatch.astype(jnp.bfloat16), quadratic_mean_mistake, pattern_agreement)


def solution(mesh):
    placed = (P(None, "lat", "lon"), P(None, "lat", "lon"), P(None, "lat", "lon"))
    return jax.shard_map(
        local,
        mesh=mesh,
        in_specs=placed,
        out_specs=(P(None, "lat", "lon"), P(), P()),
        check_vma=False,
    )
```

profile of v0, /device:TPU:0, one launch (start us, length us, event | category | flops | bytes accessed | tf_op | source)
XLA Modules:
  0.0 139.8 jit_solution(17298895487577244605)
XLA Ops:
  0.6 4.5 %copy.6 = bf16[222,40,128]{0,1,2:T(8,128)(2,1)S(1)} copy(bf16[222,40,128]{2,1,0:T(8,128)(2,1)} %param.3) | data formatting | bytes 4546560 | tf_op args[0]
  5.1 5.2 %copy.7 = bf16[222,40,128]{0,1,2:T(8,128)(2,1)} copy(bf16[222,40,128]{2,1,0:T(8,128)(2,1)} %param.4) | data formatting | bytes 4546560 | tf_op args[1]
  10.3 5.3 %copy.8 = bf16[222,40,128]{0,1,2:T(8,128)(2,1)} copy(bf16[222,40,128]{2,1,0:T(8,128)(2,1)} %param.5) | data formatting | bytes 4546560 | tf_op args[2]
  15.6 3.1 %pad_maximum_fusion.3 = (bf16[3,222,1,128]{1,2,3,0:T(2,128)(2,1)}, bf16[3,222,1,128]{1,2,3,0:T(2,128)(2,1)}) fusion(bf16[1,222,40,128]{1,2,3,0:T(8,128)(2,1)} %bitcast.25, bf16[1,222,40,128]{1,2,3,0:T(8,128)(2,1)} %bitcast.22, bf16[1,222,40,128]{1,2,3,0:T(8,128)(2,1)S(1)} %bitcast.19), kind=kLoop, calls=%fused_computation.30 | loop fusion | flops 1022976 | bytes 7160832 | tf_op jit(solution)/shard_map/slice | solution.py:13
  18.7 3.0 %collective-permute-start = (bf16[3,222,1,128]{1,2,3,0:T(2,128)(2,1)}, bf16[3,222,1,128]{1,2,3,0:T(2,128)(2,1)S(1)}, u32[]{:S(2)}, u32[]{:S(2)}) collective-permute-start(bf16[3,222,1,128]{1,2,3,0:T(2,128)(2,1)} %get-tuple-element.18), channel_id=1, source_target_pairs={{0,4},{4,8},{8,12},{12,16},{16,20},{20,24},{24,28},{28,0},{1,5},{5... | collective-permute-start | bytes 511496 | tf_op jit(solution)/shard_map/ppermute | solution.py:16
  21.7 3.0 %collective-permute-start.1 = (bf16[3,222,1,128]{1,2,3,0:T(2,128)(2,1)}, bf16[3,222,1,128]{1,2,3,0:T(2,128)(2,1)S(1)}, u32[]{:S(2)}, u32[]{:S(2)}) collective-permute-start(bf16[3,222,1,128]{1,2,3,0:T(2,128)(2,1)} %get-tuple-element.19), channel_id=1, source_target_pairs={{4,0},{8,4},{12,8},{16,12},{20,16},{24,20},{28,24},{0,28},{5,1},{9... | collective-permute-start | bytes 511496 | tf_op jit(solution)/shard_map/ppermute | solution.py:18
  24.8 0.7 fusion.11
  26.1 0.5 fusion.19
  26.6 0.6 fusion.10
  27.2 11.6 %collective-permute-done = bf16[3,222,1,128]{1,2,3,0:T(2,128)(2,1)S(1)} collective-permute-done((bf16[3,222,1,128]{1,2,3,0:T(2,128)(2,1)}, bf16[3,222,1,128]{1,2,3,0:T(2,128)(2,1)S(1)}, u32[]{:S(2)}, u32[]{:S(2)}) %collective-permute-start) | collective-permute-done | bytes 170528 | tf_op jit(solution)/shard_map/ppermute | solution.py:16
  38.8 2.1 %collective-permute-done.1 = bf16[3,222,1,128]{1,2,3,0:T(2,128)(2,1)S(1)} collective-permute-done((bf16[3,222,1,128]{1,2,3,0:T(2,128)(2,1)}, bf16[3,222,1,128]{1,2,3,0:T(2,128)(2,1)S(1)}, u32[]{:S(2)}, u32[]{:S(2)}) %collective-permute-start.1) | collective-permute-done | bytes 170528 | tf_op jit(solution)/shard_map/ppermute | solution.py:18
  40.9 1.5 %pad_maximum_fusion.8 = (bf16[3,222,42,1]{1,2,3,0:T(8,128)(2,1)}, bf16[3,222,42,1]{1,2,3,0:T(8,128)(2,1)}) fusion(bf16[3,222,1,128]{1,2,3,0:T(2,128)(2,1)S(1)} %collective-permute-done.1, bf16[3,222,1,128]{1,2,3,0:T(2,128)(2,1)S(1)} %collective-permute-done, bf16[1,222,40,128]{1,2,3,0:T(8,128)(2,1)} %bitcast.26, bf16[1,222,40,128]{1,2,3,0:T(8,128)(2,1)} %bitcast.23, ...), kind=kLoop, calls=%fused_computation.35 | loop fusion | flops 559440 | bytes 7272720 | tf_op jit(solution)/shard_map/slice | solution.py:13
  42.4 0.0 collective-permute-start.2
  42.4 1.7 %collective-permute-start.3 = (bf16[3,222,42,1]{1,2,3,0:T(8,128)(2,1)}, bf16[3,222,42,1]{1,2,3,0:T(8,128)(2,1)S(1)}, u32[]{:S(2)}, u32[]{:S(2)}) collective-permute-start(bf16[3,222,42,1]{1,2,3,0:T(8,128)(2,1)} %get-tuple-element.17), channel_id=1, source_target_pairs={{1,0},{2,1},{3,2},{0,3},{5,4},{6,5},{7,6},{4,7},{9,8},{10,9},{11,1... | collective-permute-start | bytes 167840 | tf_op jit(solution)/shard_map/ppermute | solution.py:18
  44.2 0.5 and_convert_fusion
  44.7 0.7 dynamic_slice.3
  45.4 0.0 copy-start.1
  45.4 1.0 collective-permute-done.2
  46.4 0.1 collective-permute-done.3
  46.5 10.1 %pad_maximum_fusion = bf16[3,222,42,130]{1,2,3,0:T(8,128)(2,1)S(1)} fusion(bf16[3,222,42,1]{1,2,3,0:T(8,128)(2,1)S(1)} %collective-permute-done.3, bf16[3,222,1,128]{1,2,3,0:T(2,128)(2,1)S(1)} %collective-permute-done.1, bf16[1,222,40,128]{1,2,3,0:T(8,128)(2,1)} %bitcast.27, bf16[1,222,40,128]{1,2,3,0:T(8,128)(2,1)} %bitcast.24, ...), kind=kLoop, calls=%fused_computation | loop fusion | flops 50909040 | bytes 14545440 | tf_op jit(solution)/shard_map/concatenate | solution.py:14
  56.6 0.0 copy-done.1
  56.6 5.5 %fusion.1 = (f32[222,42,130]{0,1,2:T(8,128)}, f32[222,42,130]{0,1,2:T(8,128)}) fusion(bf16[3,222,42,130]{1,2,3,0:T(8,128)(2,1)S(1)} %pad_maximum_fusion, f32[42]{0:T(128)S(1)} %copy-done.1), kind=kLoop, calls=%fused_computation.10 | loop fusion | flops 8484840 | bytes 16969848 | tf_op jit(solution)/shard_map/mul | solution.py:65
  62.1 0.0 copy-start
  62.1 16.3 %slice_add_fusion = (f32[222,40,130]{0,1,2:T(8,128)S(1)}, f32[222,40,130]{0,1,2:T(8,128)}) fusion(f32[222,42,130]{0,1,2:T(8,128)} %get-tuple-element.15, f32[222,42,130]{0,1,2:T(8,128)} %get-tuple-element.14), kind=kLoop, calls=%fused_computation.13 | loop fusion | flops 4617600 | bytes 36940800 | tf_op jit(solution)/shard_map/add | solution.py:34
  78.4 0.0 copy-done
  78.4 12.7 %fusion.5 = (f32[222]{0:T(256)S(1)}, f32[222]{0:T(256)S(1)}, f32[222]{0:T(256)S(1)}, f32[222]{0:T(256)S(1)}, f32[222]{0:T(256)S(1)}, /*index=5*/f32[222]{0:T(256...) fusion(f32[40]{0:T(128)S(1)} %dynamic_slice.3, f32[40]{0:T(128)S(1)} %copy-done, f32[222,40,130]{0,1,2:T(8,128)S(1)} %get-tuple-element.22, ...), kind=kLoop, calls=%fused_computation.18 | loop fusion | flops 22731468 | bytes 36378128 | tf_op jit(solution)/shard_map/reduce_sum | solution.py:90
  91.1 39.4 %psum.7 = f32[6,222]{1,0:T(8,128)S(1)} all-reduce(f32[6,222]{1,0:T(8,128)S(1)} %stack.43), channel_id=1, replica_groups=mesh['lat'=8,'lon'=4] {'lat','lon'}, use_global_device_ids=true, to_apply=%region_7.0 | all-reduce | flops 1332 | bytes 10656 | tf_op jit(solution)/shard_map/psum | solution.py:93
  130.5 0.6 fusion.15
  131.1 4.9 %subtract_convert_fusion = bf16[222,40,128]{0,1,2:T(8,128)(2,1)S(1)} fusion(f32[222,40,128]{0,1,2:T(8,128)} %get-tuple-element.13, f32[222,40,128]{0,1,2:T(8,128)} %get-tuple-element.12), kind=kLoop, calls=%fused_computation.27 | loop fusion | flops 2273280 | bytes 11366400 | tf_op jit(solution)/shard_map/convert_element_type | solution.py:97
  136.0 3.8 %copy.9 = bf16[222,40,128]{2,1,0:T(8,128)(2,1)} copy(bf16[222,40,128]{0,1,2:T(8,128)(2,1)S(1)} %subtract_convert_fusion) | data formatting | bytes 4546560
  (1 shorter events, 0.0 us)
Async XLA Ops:
  18.7 20.1 %collective-permute-start = (bf16[3,222,1,128]{1,2,3,0:T(2,128)(2,1)}, bf16[3,222,1,128]{1,2,3,0:T(2,128)(2,1)S(1)}, u32[]{:S(2)}, u32[]{:S(2)}) collective-permute-start(bf16[3,222,1,128]{1,2,3,0:T(2,128)(2,1)} %get-tuple-element.18), channel_id=1, source_target_pairs={{0,4},{4,8},{8,12},{12,16},{16,20},{20,24},{24,28},{28,0},{1,5},{5... | collective-permute-start | bytes 511496 | tf_op jit(solution)/shard_map/ppermute | solution.py:16
  21.7 19.2 %collective-permute-start.1 = (bf16[3,222,1,128]{1,2,3,0:T(2,128)(2,1)}, bf16[3,222,1,128]{1,2,3,0:T(2,128)(2,1)S(1)}, u32[]{:S(2)}, u32[]{:S(2)}) collective-permute-start(bf16[3,222,1,128]{1,2,3,0:T(2,128)(2,1)} %get-tuple-element.19), channel_id=1, source_target_pairs={{4,0},{8,4},{12,8},{16,12},{20,16},{24,20},{28,24},{0,28},{5,1},{9... | collective-permute-start | bytes 511496 | tf_op jit(solution)/shard_map/ppermute | solution.py:18
  42.4 4.0 %collective-permute-start.2 = (bf16[3,222,42,1]{1,2,3,0:T(8,128)(2,1)}, bf16[3,222,42,1]{1,2,3,0:T(8,128)(2,1)S(1)}, u32[]{:S(2)}, u32[]{:S(2)}) collective-permute-start(bf16[3,222,42,1]{1,2,3,0:T(8,128)(2,1)} %get-tuple-element.16), channel_id=1, source_target_pairs={{0,1},{1,2},{2,3},{3,0},{4,5},{5,6},{6,7},{7,4},{8,9},{9,10},{10,1... | collective-permute-start | bytes 167840 | tf_op jit(solution)/shard_map/ppermute | solution.py:16
  42.4 4.0 %collective-permute-start.3 = (bf16[3,222,42,1]{1,2,3,0:T(8,128)(2,1)}, bf16[3,222,42,1]{1,2,3,0:T(8,128)(2,1)S(1)}, u32[]{:S(2)}, u32[]{:S(2)}) collective-permute-start(bf16[3,222,42,1]{1,2,3,0:T(8,128)(2,1)} %get-tuple-element.17), channel_id=1, source_target_pairs={{1,0},{2,1},{3,2},{0,3},{5,4},{6,5},{7,6},{4,7},{9,8},{10,9},{11,1... | collective-permute-start | bytes 167840 | tf_op jit(solution)/shard_map/ppermute | solution.py:18
  45.4 11.1 %copy-start.1 = (f32[42]{0:T(128)S(1)}, f32[42]{0:T(128)}, u32[]{:S(2)}) copy-start(f32[42]{0:T(128)} %and_convert_fusion) | copy-start | bytes 508
  62.1 16.3 %copy-start = (f32[40]{0:T(128)S(1)}, f32[40]{0:T(128)}, u32[]{:S(2)}) copy-start(f32[40]{0:T(128)} %fusion.19) | copy-start | bytes 484
where the time goes:
time: 140 us
  other arithmetic  57 us (41%)
  blocking collectives  39.4 us (28%)
  local copies, waits for them, and re-layouts  19.5 us (14%)
  waiting for transfers between devices  14.7 us (10%)
  starting transfers between devices  7.78 us (6%)
    psum x1, blocking collectives, local(): totals = lax.psum(running_accumulations, ('lat', 'lon'))  39.4 us
    unnamed x8, local copies, waits for them, and re-layouts  18.7 us
    add x1, other arithmetic, vertical_sum(): return member[:, :-2] + member[:, 1:-1] + member[:, 2:]  16.3 us
    reduce_sum x1, other arithmetic, local(): jnp.sum(weighted_fcst * averaged_observation, axis=(1, 2))  12.7 us
    ppermute x2, waiting for transfers between devices, extended(): lax.ppermute(tail, axis, [(i, (i + 1) % count) for i in range(count)])  12.6 us
    concatenate x1, other arithmetic, extended(): jnp.concatenate([lax.ppermute(tail, axis, [(i, (i + 1) % count) for i in...  10.1 us
    mul x1, other arithmetic, local(): member * inside  5.51 us
    convert_element_type x1, other arithmetic, local(): prediction_mismatch.astype(jnp.bfloat16)  4.93 us
  transfers between devices with their start and end apart: 4, of which 4 were waited for; matrix products, arithmetic and copies ran while one was open for 2% of the time, Pallas kernels for 0%

commit v1 on v0

--- a/solution.py
+++ b/solution.py
@@ -90,7 +90,7 @@
             jnp.sum(weighted_fcst * averaged_observation, axis=(1, 2)),
         ]
     )
-    totals = lax.psum(running_accumulations, ("lat", "lon"))
+    totals = lax.psum(lax.psum(running_accumulations, "lat"), "lon")
     quadratic_mean_mistake, pattern_agreement = finish(
         totals, float(parallel_overall_accumulated * meridian_accumulated)
     )

time: 140 us -> 127 us (0.907)
  blocking collectives: 39.4 us -> 26.5 us
    psum x1 -> x2, blocking collectives: 39.4 us -> 26.5 us  [local(): totals = lax.psum(lax.psum(running_accumulations, 'lat'), 'lon')]
where the time goes in v1:
time: 127 us
  other arithmetic  57 us (45%)
  blocking collectives  26.5 us (21%)
  local copies, waits for them, and re-layouts  19.5 us (15%)
  waiting for transfers between devices  14.7 us (12%)
  starting transfers between devices  7.78 us (6%)
  between operations  1.34 us (1%)
    psum x2, blocking collectives, local(): totals = lax.psum(lax.psum(running_accumulations, 'lat'), 'lon')  26.5 us
    unnamed x8, local copies, waits for them, and re-layouts  18.7 us
    add x1, other arithmetic, vertical_sum(): return member[:, :-2] + member[:, 1:-1] + member[:, 2:]  16.3 us
    reduce_sum x1, other arithmetic, local(): jnp.sum(weighted_fcst * averaged_observation, axis=(1, 2))  12.7 us
    ppermute x2, waiting for transfers between devices, extended(): lax.ppermute(tail, axis, [(i, (i + 1) % count) for i in range(count)])  12.6 us
    concatenate x1, other arithmetic, extended(): jnp.concatenate([lax.ppermute(tail, axis, [(i, (i + 1) % count) for i in...  10.1 us
    mul x1, other arithmetic, local(): member * inside  5.51 us
    convert_element_type x1, other arithmetic, local(): prediction_mismatch.astype(jnp.bfloat16)  4.93 us
  transfers between devices with their start and end apart: 4, of which 4 were waited for; matrix products, arithmetic and copies ran while one was open for 2% of the time, Pallas kernels for 0%

profile of v1, /device:TPU:0, one launch (start us, length us, event | category | flops | bytes accessed | tf_op | source)
XLA Modules:
  0.0 126.9 jit_solution(17834801807765138627)
XLA Ops:
  0.6 4.5 %copy.6 = bf16[222,40,128]{0,1,2:T(8,128)(2,1)S(1)} copy(bf16[222,40,128]{2,1,0:T(8,128)(2,1)} %param.3) | data formatting | bytes 4546560 | tf_op args[0]
  5.1 5.2 %copy.7 = bf16[222,40,128]{0,1,2:T(8,128)(2,1)} copy(bf16[222,40,128]{2,1,0:T(8,128)(2,1)} %param.4) | data formatting | bytes 4546560 | tf_op args[1]
  10.3 5.3 %copy.8 = bf16[222,40,128]{0,1,2:T(8,128)(2,1)} copy(bf16[222,40,128]{2,1,0:T(8,128)(2,1)} %param.5) | data formatting | bytes 4546560 | tf_op args[2]
  15.6 3.1 %pad_maximum_fusion.3 = (bf16[3,222,1,128]{1,2,3,0:T(2,128)(2,1)}, bf16[3,222,1,128]{1,2,3,0:T(2,128)(2,1)}) fusion(bf16[1,222,40,128]{1,2,3,0:T(8,128)(2,1)} %bitcast.25, bf16[1,222,40,128]{1,2,3,0:T(8,128)(2,1)} %bitcast.22, bf16[1,222,40,128]{1,2,3,0:T(8,128)(2,1)S(1)} %bitcast.19), kind=kLoop, calls=%fused_computation.30 | loop fusion | flops 1022976 | bytes 7160832 | tf_op jit(solution)/shard_map/slice | solution.py:13
  18.7 3.0 %collective-permute-start = (bf16[3,222,1,128]{1,2,3,0:T(2,128)(2,1)}, bf16[3,222,1,128]{1,2,3,0:T(2,128)(2,1)S(1)}, u32[]{:S(2)}, u32[]{:S(2)}) collective-permute-start(bf16[3,222,1,128]{1,2,3,0:T(2,128)(2,1)} %get-tuple-element.18), channel_id=1, source_target_pairs={{0,4},{4,8},{8,12},{12,16},{16,20},{20,24},{24,28},{28,0},{1,5},{5... | collective-permute-start | bytes 511496 | tf_op jit(solution)/shard_map/ppermute | solution.py:16
  21.7 3.0 %collective-permute-start.1 = (bf16[3,222,1,128]{1,2,3,0:T(2,128)(2,1)}, bf16[3,222,1,128]{1,2,3,0:T(2,128)(2,1)S(1)}, u32[]{:S(2)}, u32[]{:S(2)}) collective-permute-start(bf16[3,222,1,128]{1,2,3,0:T(2,128)(2,1)} %get-tuple-element.19), channel_id=1, source_target_pairs={{4,0},{8,4},{12,8},{16,12},{20,16},{24,20},{28,24},{0,28},{5,1},{9... | collective-permute-start | bytes 511496 | tf_op jit(solution)/shard_map/ppermute | solution.py:18
  24.8 0.7 fusion.11
  26.1 0.5 fusion.19
  26.6 0.6 fusion.10
  27.2 11.6 %collective-permute-done = bf16[3,222,1,128]{1,2,3,0:T(2,128)(2,1)S(1)} collective-permute-done((bf16[3,222,1,128]{1,2,3,0:T(2,128)(2,1)}, bf16[3,222,1,128]{1,2,3,0:T(2,128)(2,1)S(1)}, u32[]{:S(2)}, u32[]{:S(2)}) %collective-permute-start) | collective-permute-done | bytes 170528 | tf_op jit(solution)/shard_map/ppermute | solution.py:16
  38.8 2.1 %collective-permute-done.1 = bf16[3,222,1,128]{1,2,3,0:T(2,128)(2,1)S(1)} collective-permute-done((bf16[3,222,1,128]{1,2,3,0:T(2,128)(2,1)}, bf16[3,222,1,128]{1,2,3,0:T(2,128)(2,1)S(1)}, u32[]{:S(2)}, u32[]{:S(2)}) %collective-permute-start.1) | collective-permute-done | bytes 170528 | tf_op jit(solution)/shard_map/ppermute | solution.py:18
  40.9 1.5 %pad_maximum_fusion.8 = (bf16[3,222,42,1]{1,2,3,0:T(8,128)(2,1)}, bf16[3,222,42,1]{1,2,3,0:T(8,128)(2,1)}) fusion(bf16[3,222,1,128]{1,2,3,0:T(2,128)(2,1)S(1)} %collective-permute-done.1, bf16[3,222,1,128]{1,2,3,0:T(2,128)(2,1)S(1)} %collective-permute-done, bf16[1,222,40,128]{1,2,3,0:T(8,128)(2,1)} %bitcast.26, bf16[1,222,40,128]{1,2,3,0:T(8,128)(2,1)} %bitcast.23, ...), kind=kLoop, calls=%fused_computation.35 | loop fusion | flops 559440 | bytes 7272720 | tf_op jit(solution)/shard_map/slice | solution.py:13
  42.4 0.0 collective-permute-start.2
  42.4 1.7 %collective-permute-start.3 = (bf16[3,222,42,1]{1,2,3,0:T(8,128)(2,1)}, bf16[3,222,42,1]{1,2,3,0:T(8,128)(2,1)S(1)}, u32[]{:S(2)}, u32[]{:S(2)}) collective-permute-start(bf16[3,222,42,1]{1,2,3,0:T(8,128)(2,1)} %get-tuple-element.17), channel_id=1, source_target_pairs={{1,0},{2,1},{3,2},{0,3},{5,4},{6,5},{7,6},{4,7},{9,8},{10,9},{11,1... | collective-permute-start | bytes 167840 | tf_op jit(solution)/shard_map/ppermute | solution.py:18
  44.2 0.5 and_convert_fusion
  44.7 0.7 dynamic_slice.3
  45.4 0.0 copy-start.1
  45.4 1.0 collective-permute-done.2
  46.4 0.1 collective-permute-done.3
  46.5 10.1 %pad_maximum_fusion = bf16[3,222,42,130]{1,2,3,0:T(8,128)(2,1)S(1)} fusion(bf16[3,222,42,1]{1,2,3,0:T(8,128)(2,1)S(1)} %collective-permute-done.3, bf16[3,222,1,128]{1,2,3,0:T(2,128)(2,1)S(1)} %collective-permute-done.1, bf16[1,222,40,128]{1,2,3,0:T(8,128)(2,1)} %bitcast.27, bf16[1,222,40,128]{1,2,3,0:T(8,128)(2,1)} %bitcast.24, ...), kind=kLoop, calls=%fused_computation | loop fusion | flops 50909040 | bytes 14545440 | tf_op jit(solution)/shard_map/concatenate | solution.py:14
  56.6 0.0 copy-done.1
  56.6 5.5 %fusion.1 = (f32[222,42,130]{0,1,2:T(8,128)}, f32[222,42,130]{0,1,2:T(8,128)}) fusion(bf16[3,222,42,130]{1,2,3,0:T(8,128)(2,1)S(1)} %pad_maximum_fusion, f32[42]{0:T(128)S(1)} %copy-done.1), kind=kLoop, calls=%fused_computation.10 | loop fusion | flops 8484840 | bytes 16969848 | tf_op jit(solution)/shard_map/mul | solution.py:65
  62.1 0.0 copy-start
  62.1 16.3 %slice_add_fusion = (f32[222,40,130]{0,1,2:T(8,128)S(1)}, f32[222,40,130]{0,1,2:T(8,128)}) fusion(f32[222,42,130]{0,1,2:T(8,128)} %get-tuple-element.15, f32[222,42,130]{0,1,2:T(8,128)} %get-tuple-element.14), kind=kLoop, calls=%fused_computation.13 | loop fusion | flops 4617600 | bytes 36940800 | tf_op jit(solution)/shard_map/add | solution.py:34
  78.4 0.0 copy-done
  78.4 12.7 %fusion.5 = (f32[222]{0:T(256)S(1)}, f32[222]{0:T(256)S(1)}, f32[222]{0:T(256)S(1)}, f32[222]{0:T(256)S(1)}, f32[222]{0:T(256)S(1)}, /*index=5*/f32[222]{0:T(256...) fusion(f32[40]{0:T(128)S(1)} %dynamic_slice.3, f32[40]{0:T(128)S(1)} %copy-done, f32[222,40,130]{0,1,2:T(8,128)S(1)} %get-tuple-element.22, ...), kind=kLoop, calls=%fused_computation.18 | loop fusion | flops 22731468 | bytes 36378128 | tf_op jit(solution)/shard_map/reduce_sum | solution.py:90
  91.1 20.7 %psum.14 = f32[6,222]{1,0:T(8,128)S(1)} all-reduce(f32[6,222]{1,0:T(8,128)S(1)} %stack.43), channel_id=1, replica_groups=mesh['lat'=8,'lon'=4] {'lat'}, use_global_device_ids=true, to_apply=%region_7.0 | all-reduce | flops 1332 | bytes 10656 | tf_op jit(solution)/shard_map/psum | solution.py:93
  111.8 5.8 %psum.15 = f32[6,222]{1,0:T(8,128)S(1)} all-reduce(f32[6,222]{1,0:T(8,128)S(1)} %psum.14), channel_id=1, replica_groups=mesh['lat'=8,'lon'=4] {'lon'}, use_global_device_ids=true, to_apply=%region_8.0 | all-reduce | flops 1332 | bytes 10656 | tf_op jit(solution)/shard_map/psum | solution.py:93
  117.6 0.6 fusion.15
  118.1 4.9 %subtract_convert_fusion = bf16[222,40,128]{0,1,2:T(8,128)(2,1)S(1)} fusion(f32[222,40,128]{0,1,2:T(8,128)} %get-tuple-element.13, f32[222,40,128]{0,1,2:T(8,128)} %get-tuple-element.12), kind=kLoop, calls=%fused_computation.27 | loop fusion | flops 2273280 | bytes 11366400 | tf_op jit(solution)/shard_map/convert_element_type | solution.py:97
  123.1 3.8 %copy.9 = bf16[222,40,128]{2,1,0:T(8,128)(2,1)} copy(bf16[222,40,128]{0,1,2:T(8,128)(2,1)S(1)} %subtract_convert_fusion) | data formatting | bytes 4546560
  (1 shorter events, 0.0 us)
Async XLA Ops:
  18.7 20.1 %collective-permute-start = (bf16[3,222,1,128]{1,2,3,0:T(2,128)(2,1)}, bf16[3,222,1,128]{1,2,3,0:T(2,128)(2,1)S(1)}, u32[]{:S(2)}, u32[]{:S(2)}) collective-permute-start(bf16[3,222,1,128]{1,2,3,0:T(2,128)(2,1)} %get-tuple-element.18), channel_id=1, source_target_pairs={{0,4},{4,8},{8,12},{12,16},{16,20},{20,24},{24,28},{28,0},{1,5},{5... | collective-permute-start | bytes 511496 | tf_op jit(solution)/shard_map/ppermute | solution.py:16
  21.7 19.2 %collective-permute-start.1 = (bf16[3,222,1,128]{1,2,3,0:T(2,128)(2,1)}, bf16[3,222,1,128]{1,2,3,0:T(2,128)(2,1)S(1)}, u32[]{:S(2)}, u32[]{:S(2)}) collective-permute-start(bf16[3,222,1,128]{1,2,3,0:T(2,128)(2,1)} %get-tuple-element.19), channel_id=1, source_target_pairs={{4,0},{8,4},{12,8},{16,12},{20,16},{24,20},{28,24},{0,28},{5,1},{9... | collective-permute-start | bytes 511496 | tf_op jit(solution)/shard_map/ppermute | solution.py:18
  42.4 4.0 %collective-permute-start.2 = (bf16[3,222,42,1]{1,2,3,0:T(8,128)(2,1)}, bf16[3,222,42,1]{1,2,3,0:T(8,128)(2,1)S(1)}, u32[]{:S(2)}, u32[]{:S(2)}) collective-permute-start(bf16[3,222,42,1]{1,2,3,0:T(8,128)(2,1)} %get-tuple-element.16), channel_id=1, source_target_pairs={{0,1},{1,2},{2,3},{3,0},{4,5},{5,6},{6,7},{7,4},{8,9},{9,10},{10,1... | collective-permute-start | bytes 167840 | tf_op jit(solution)/shard_map/ppermute | solution.py:16
  42.4 4.0 %collective-permute-start.3 = (bf16[3,222,42,1]{1,2,3,0:T(8,128)(2,1)}, bf16[3,222,42,1]{1,2,3,0:T(8,128)(2,1)S(1)}, u32[]{:S(2)}, u32[]{:S(2)}) collective-permute-start(bf16[3,222,42,1]{1,2,3,0:T(8,128)(2,1)} %get-tuple-element.17), channel_id=1, source_target_pairs={{1,0},{2,1},{3,2},{0,3},{5,4},{6,5},{7,6},{4,7},{9,8},{10,9},{11,1... | collective-permute-start | bytes 167840 | tf_op jit(solution)/shard_map/ppermute | solution.py:18
  45.4 11.1 %copy-start.1 = (f32[42]{0:T(128)S(1)}, f32[42]{0:T(128)}, u32[]{:S(2)}) copy-start(f32[42]{0:T(128)} %and_convert_fusion) | copy-start | bytes 508
  62.1 16.3 %copy-start = (f32[40]{0:T(128)S(1)}, f32[40]{0:T(128)}, u32[]{:S(2)}) copy-start(f32[40]{0:T(128)} %fusion.19) | copy-start | bytes 484
